TPU v7x, 512 devices: a whole 4x8x8 slice. The times are simulated.
512 devices in a mesh: row: 32 (over y_lo, x, core), col: 8 (over z), dp: 2 (over y_hi).
Axes of the slice: x: 4, y: 8 (y_hi: 2, y_lo: 4; y = y_hi * 4 + y_lo), z: 8, core: 2. Of those that a mesh axis runs over, the one named last changes fastest.
Arguments:
- pixels: bfloat16 [2, 3, 1024, 1024], P('dp', None, 'row', 'col'), may hold values from -6 to 6
- cotangent: bfloat16 [2, 256, 256, 1024], P('dp', 'row', 'col'), may hold values from -6 to 6
- embed_weight: bfloat16 [48, 1024], replicated, may hold values from -0.875 to 0.875
- embed_bias: float32 [1024], replicated, may hold values from -4 to 4
- layer_norm_gain: float32 [1024], replicated, may hold values from 0.5 to 1.5
- qkv_weight: bfloat16 [1024, 2304], P('row', ('col', 'dp')), may hold values from -0.1875 to 0.1875
- out_weight: bfloat16 [768, 1024], P('row', ('col', 'dp')), may hold values from -0.21875 to 0.21875
- bias_table: float32 [12, 225], replicated, may hold values from -4 to 404
- rel_index: int32 [64, 64], replicated, may hold values from 0 to 224
- shifts: int32 [2, 2], P('dp'), may hold values from 1 to 7
Outputs:
- out_weight_grad: float32 [768, 1024], P('row', ('col', 'dp'))
- embed_weight_grad: float32 [48, 1024], replicated
- embed_bias_grad: float32 [1024], replicated
- norm_gain_grad: float32 [1024], replicated
- bias_table_grad: float32 [12, 225], replicated
Inputs may be any that keep to these rules, and one draw needn't show every extreme that they name: `rel_index`: each entry names one of the 225 columns of bias_table.
All inputs are finite; a program needn't handle non-finite values.
Results may differ from a plain program's by a relative error of at most 0.023.
Values may be sent and summed in bfloat16 or wider, within the bound.
No kernel may reach another device: no remote copies, remote signals or barrier semaphores. Data moves between devices by JAX's collectives and lax.ppermute only.
A program may use at most 64 MiB of HBM per device.

v0:
```python
import jax
import jax.numpy as jnp
from jax import lax
from jax.sharding import PartitionSpec as P

WIN = 8
PATCH = 4
norm_epsilon = 1e-05


def laid_out(blocks, dim):
    blocks = jnp.moveaxis(blocks, 0, dim)
    lengths = blocks.shape
    return blocks.reshape(*lengths[:dim], lengths[dim] * lengths[dim + 1], *lengths[dim + 2 :])


def gather_together(arrays, axis, dims):
    line = jnp.concatenate([a.reshape(-1) for a in arrays])
    lines, at, gathered = (lax.all_gather(line, axis), 0, [])
    for a, dim in zip(arrays, dims):
        blocks = lines[:, at : at + a.size].reshape(-1, *a.shape)
        gathered.append(laid_out(blocks, dim))
        at += a.size
    return tuple(gathered)


def from_behind(value, axis, steps):
    count = lax.axis_size(axis)
    pairs = [(source, (source + steps) % count) for source in range(count)]
    return lax.ppermute(value, axis, pairs)


def in_blocks(x, dim, length):
    before, after = (x.shape[:dim], x.shape[dim + 1 :])
    return jnp.moveaxis(x.reshape(*before, length, -1, *after), dim, 0)


def summed_on_arrival(x, axis, dim):
    blocks = in_blocks(x, dim, lax.axis_size(axis))
    arrived = lax.all_to_all(blocks, axis, split_axis=0, concat_axis=0, tiled=True)
    return arrived.astype(jnp.float32).sum(axis=0)


def summed_on_arrival_2(x, axis, dim):
    blocks = in_blocks(x, dim, lax.axis_size(axis))
    arrived = lax.all_to_all(blocks, axis, split_axis=0, concat_axis=0, tiled=True)
    return arrived.sum(axis=0)


def make_patches(pixel_block):
    images, channels, pixel_rows, pixel_cols = pixel_block.shape
    grid_rows = pixel_rows // PATCH
    grid_cols = pixel_cols // PATCH
    shaped = pixel_block.reshape(images, channels, grid_rows, PATCH, grid_cols, PATCH)
    return shaped.transpose(0, 2, 4, 1, 3, 5).reshape(
        images, grid_rows, grid_cols, channels * PATCH * PATCH
    )


def embed_cells(patches, embed_weight, embed_bias):
    return (jnp.dot(patches, embed_weight, preferred_element_type=jnp.float32) + embed_bias).astype(
        jnp.bfloat16
    )


def window_split(block):
    rows_all, cols_all, features = block.shape
    shaped = block.reshape(rows_all // WIN, WIN, cols_all // WIN, WIN, features)
    return shaped.transpose(0, 2, 1, 3, 4).reshape(-1, WIN * WIN, features)


def window_join(windows, rows_all, cols_all):
    features = windows.shape[-1]
    shaped = windows.reshape(rows_all // WIN, cols_all // WIN, WIN, WIN, features)
    return shaped.transpose(0, 2, 1, 3, 4).reshape(rows_all, cols_all, features)


def splice_after(own_block, borrowed, offsets, along_dim):
    length = own_block.shape[along_dim]

    def single(own_item, borrowed_item, offset):
        joined = jnp.concatenate([own_item, borrowed_item], along_dim - 1)
        return lax.dynamic_slice_in_dim(joined, offset, length, along_dim - 1)

    return jax.vmap(single)(own_block, borrowed, offsets)


def attend_forward(cell_windows, labels, layer_norm_gain, qkv_full, bias_full):
    window_count, cell_count, features = cell_windows.shape
    head_count = bias_full.shape[0]
    inner_width = qkv_full.shape[1] // 3
    head_size = inner_width // head_count
    score_scale = head_size ** (-0.5)
    flat_rows = cell_windows.reshape(-1, features).astype(jnp.float32)
    average = jnp.mean(flat_rows, axis=-1, keepdims=True)
    centered_input = flat_rows - average
    inverse_deviation = lax.rsqrt(
        jnp.mean(centered_input * centered_input, axis=-1, keepdims=True) + norm_epsilon
    )
    standardized_rows = centered_input * inverse_deviation
    normalized_rows = (standardized_rows * layer_norm_gain).astype(jnp.bfloat16)
    projected = jnp.dot(normalized_rows, qkv_full, preferred_element_type=jnp.float32).astype(
        jnp.bfloat16
    )
    head_shape = (window_count, cell_count, head_count, head_size)
    query_rows = projected[:, :inner_width].reshape(head_shape)
    key_vectors = projected[:, inner_width : 2 * inner_width].reshape(head_shape)
    value_rows = projected[:, 2 * inner_width :].reshape(head_shape)
    scores = (
        jnp.einsum("wmhd,wnhd->whmn", query_rows, key_vectors, preferred_element_type=jnp.float32)
        * score_scale
        + bias_full[None]
    )
    same_region = labels[:, None, :, None] == labels[:, None, None, :]
    scores = jnp.where(same_region, scores, -1e30)
    row_peak = jnp.max(scores, axis=-1, keepdims=True)
    exp_scores = jnp.exp(scores - row_peak)
    attention_weights = exp_scores / jnp.sum(exp_scores, axis=-1, keepdims=True)
    reduced_probability = attention_weights.astype(jnp.bfloat16)
    attended = jnp.einsum(
        "whmn,wnhd->wmhd", reduced_probability, value_rows, preferred_element_type=jnp.float32
    ).astype(jnp.bfloat16)
    stored_residuals = (
        standardized_rows,
        inverse_deviation,
        query_rows,
        key_vectors,
        value_rows,
        attention_weights,
        reduced_probability,
    )
    return (stored_residuals, attended.reshape(-1, inner_width))


def attend_backward(stored_residuals, d_attended, layer_norm_gain, qkv_full):
    (
        standardized_rows,
        inverse_deviation,
        query_rows,
        key_vectors,
        value_rows,
        attention_weights,
        reduced_probability,
    ) = stored_residuals
    head_shape = query_rows.shape
    score_scale = head_shape[3] ** (-0.5)
    total_row_count = standardized_rows.shape[0]
    inner_width = head_shape[2] * head_shape[3]
    d_heads = d_attended.reshape(head_shape)
    d_prob = jnp.einsum("wmhd,wnhd->whmn", d_heads, value_rows, preferred_element_type=jnp.float32)
    d_values = jnp.einsum(
        "whmn,wmhd->wnhd", reduced_probability, d_heads, preferred_element_type=jnp.float32
    ).astype(jnp.bfloat16)
    d_scores = attention_weights * (
        d_prob - jnp.sum(attention_weights * d_prob, axis=-1, keepdims=True)
    )
    table_part = jnp.sum(d_scores, axis=0)
    d_low = d_scores.astype(jnp.bfloat16)
    d_queries = (
        jnp.einsum("whmn,wnhd->wmhd", d_low, key_vectors, preferred_element_type=jnp.float32)
        * score_scale
    ).astype(jnp.bfloat16)
    d_keys = (
        jnp.einsum("whmn,wmhd->wnhd", d_low, query_rows, preferred_element_type=jnp.float32)
        * score_scale
    ).astype(jnp.bfloat16)
    d_projected = jnp.concatenate(
        [
            d_queries.reshape(total_row_count, inner_width),
            d_keys.reshape(total_row_count, inner_width),
            d_values.reshape(total_row_count, inner_width),
        ],
        axis=1,
    )
    normalized_gradient = lax.dot_general(
        d_projected, qkv_full, (((1,), (1,)), ((), ())), preferred_element_type=jnp.float32
    )
    gain_contribution = jnp.sum(normalized_gradient * standardized_rows, axis=0)
    scaled_rows = normalized_gradient * layer_norm_gain
    branch_gradient = inverse_deviation * (
        scaled_rows
        - jnp.mean(scaled_rows, axis=-1, keepdims=True)
        - standardized_rows * jnp.mean(scaled_rows * standardized_rows, axis=-1, keepdims=True)
    )
    return (branch_gradient.astype(jnp.bfloat16), gain_contribution, table_part)


def on_device(
    pixels,
    cotangent,
    embed_weight,
    embed_bias,
    layer_norm_gain,
    qkv_weight,
    out_weight,
    bias_table,
    rel_index,
    shifts,
):
    images, rows_dev, cols_dev, features = cotangent.shape
    head_count = bias_table.shape[0]
    grid_rows = rows_dev * lax.axis_size("row")
    grid_cols = cols_dev * lax.axis_size("col")
    row_shift = shifts[:, 0]
    col_shift = shifts[:, 1]
    qkv_columns, out_columns = gather_together((qkv_weight, out_weight), ("col", "dp"), (1, 1))
    qkv_full = lax.all_gather(qkv_columns, "row", axis=0, tiled=True)
    patches = make_patches(pixels)
    below = from_behind((pixels, cotangent), "row", -1)
    moved_pixels = splice_after(pixels, below[0], row_shift * PATCH, 2)
    shifted_cot = splice_after(cotangent, below[1], row_shift, 1)
    beside = from_behind((moved_pixels[:, :, :, : WIN * PATCH], shifted_cot[:, :, :WIN]), "col", -1)
    moved_pixels = splice_after(moved_pixels, beside[0], col_shift * PATCH, 3)
    shifted_cot = splice_after(shifted_cot, beside[1], col_shift, 2)
    moved_patches = make_patches(moved_pixels)
    shifted = embed_cells(moved_patches, embed_weight, embed_bias)
    row_ids = lax.axis_index("row") * rows_dev + jnp.arange(rows_dev, dtype=jnp.int32)
    col_ids = lax.axis_index("col") * cols_dev + jnp.arange(cols_dev, dtype=jnp.int32)
    row_part = (row_ids[None, :] >= grid_rows - row_shift[:, None]).astype(jnp.int32)
    col_part = (col_ids[None, :] >= grid_cols - col_shift[:, None]).astype(jnp.int32)
    region = 2 * row_part[:, :, None] + col_part[:, None, :]
    labels = window_split(region.reshape(images * rows_dev, cols_dev, 1))[:, :, 0]
    cell_windows = window_split(shifted.reshape(images * rows_dev, cols_dev, features))
    cot_flat = window_split(shifted_cot.reshape(images * rows_dev, cols_dev, features)).reshape(
        -1, features
    )
    selector = (
        rel_index.reshape(-1)[:, None] == jnp.arange(bias_table.shape[1], dtype=jnp.int32)[None, :]
    ).astype(jnp.float32)
    bias_full = jnp.dot(selector, bias_table.T, precision=lax.Precision.HIGHEST).T.reshape(
        head_count, WIN * WIN, WIN * WIN
    )
    stored_residuals, attended = attend_forward(
        cell_windows, labels, layer_norm_gain, qkv_full, bias_full
    )
    d_attended = lax.dot_general(
        cot_flat,
        lax.all_gather(out_columns, "row", axis=0, tiled=True),
        (((1,), (1,)), ((), ())),
        preferred_element_type=jnp.float32,
    ).astype(jnp.bfloat16)
    partial_rows = summed_on_arrival(
        lax.dot_general(
            attended, cot_flat, (((0,), (0,)), ((), ())), preferred_element_type=jnp.float32
        ).astype(jnp.bfloat16),
        "row",
        0,
    )
    out_weight_grad = summed_on_arrival_2(partial_rows, ("col", "dp"), 1)
    d_rows, gain_contribution, table_part = attend_backward(
        stored_residuals, d_attended, layer_norm_gain, qkv_full
    )
    branch_gradient = window_join(
        d_rows.reshape(-1, WIN * WIN, features), images * rows_dev, cols_dev
    ).reshape(images, rows_dev, cols_dev, features)
    patch_rows = patches.reshape(-1, patches.shape[-1])
    cot_rows = cotangent.reshape(-1, features)
    contract = (((0,), (0,)), ((), ()))
    branch_patches = moved_patches.reshape(-1, patches.shape[-1])
    back_rows = branch_gradient.reshape(-1, features)
    embed_grad = lax.dot_general(
        patch_rows, cot_rows, contract, preferred_element_type=jnp.float32
    ) + lax.dot_general(branch_patches, back_rows, contract, preferred_element_type=jnp.float32)
    bias_grad = jnp.sum(cot_rows, axis=0, dtype=jnp.float32) + jnp.sum(
        back_rows, axis=0, dtype=jnp.float32
    )
    table_grad = jnp.dot(
        table_part.reshape(head_count, -1), selector, precision=lax.Precision.HIGHEST
    )
    totals = lax.psum((embed_grad, bias_grad, gain_contribution, table_grad), ("row", "col", "dp"))
    return (out_weight_grad, totals[0], totals[1], totals[2], totals[3])


def solution(mesh):
    return jax.shard_map(
        on_device,
        mesh=mesh,
        in_specs=(
            P("dp", None, "row", "col"),
            P("dp", "row", "col", None),
            P(),
            P(),
            P(),
            P("row", ("col", "dp")),
            P("row", ("col", "dp")),
            P(),
            P(),
            P("dp", None),
        ),
        out_specs=(P("row", ("col", "dp")), P(), P(), P(), P()),
        check_vma=False,
    )
```

profile of v0, /device:TPU:1, one launch (start us, length us, event | category | flops | bytes accessed | tf_op | source)
XLA Modules:
  0.0 531.4 jit_solution(17640539228730412857)
XLA Ops:
  8.9 54.6 %all-gather = bf16[98304]{0:T(1024)(128)(2,1)S(1)} all-gather(bf16[6144]{0:T(1024)(128)(2,1)S(1)} %pad_maximum_fusion), channel_id=2, replica_groups=mesh['row'=32,'col'=8,'dp'=2] {'col','dp'}, dimensions={0}, use_global_device_ids=true | all-gather | bytes 208896 | tf_op jit(solution)/shard_map/all_gather | solution.py:19
  65.3 10.1 %collective-permute-start = (bf16[1,3,32,128]{3,2,1,0:T(8,128)(2,1)S(1)}, bf16[1,3,32,128]{3,2,1,0:T(8,128)(2,1)S(1)}, u32[]{:S(2)}, u32[]{:S(2)}) collective-permute-start(bf16[1,3,32,128]{3,2,1,0:T(8,128)(2,1)S(1)} %copy-done.12), channel_id=1, source_target_pairs={{0,496},{16,0},{32,16},{48,32},{64,48},{80,64},{96,80},{112,96},{1... | collective-permute-start | bytes 73736 | tf_op jit(solution)/shard_map/ppermute | solution.py:30
  75.4 1.9 collective-permute-start.2
  78.3 1.7 reshape.208
  82.9 2.6 convolution_bitcast_fusion
  87.2 1.9 collective-permute-start.1
  94.3 1.7 reshape.196
  98.8 2.1 collective-permute-start.3
  102.7 2.3 collective-permute-done.3
  106.1 26.1 %all-gather.4.cloned.1.call-done = bf16[1024,2304]{1,0:T(8,128)(2,1)} async-done(((bf16[32,2304]{1,0:T(8,128)(2,1)}), bf16[1024,2304]{1,0:T(8,128)(2,1)}) %all-gather.4.cloned.1.call-update) | async-done | bytes 4718608 | tf_op jit(solution)/shard_map/all_gather | solution.py:207
  132.1 3.9 convolution_convert_fusion
  138.5 2.6 reshape.338
  142.7 1.8 copy.192
  144.9 1.6 fusion.42
  146.5 3.8 fusion.7
  150.3 1.8 copy.179
  153.3 2.9 convolution_convert_fusion.1
  156.2 5.3 all-to-all-start
  161.4 41.0 %all-gather.6.cloned.1.call-done = bf16[768,1024]{1,0:T(8,128)(2,1)} async-done(((bf16[24,1024]{1,0:T(8,128)(2,1)}), bf16[768,1024]{1,0:T(8,128)(2,1)}) %all-gather.6.cloned.1.call-update) | async-done | bytes 1572880 | tf_op jit(solution)/shard_map/all_gather | solution.py:238
  202.5 2.8 convolution_convert_fusion.4
  205.2 2.4 reshape.341
  207.7 1.8 copy.196
  209.5 2.5 multiply_reduce_fusion
  213.3 1.9 copy.200
  215.2 1.8 reshape.216
  225.6 2.5 fusion.8
  229.3 4.0 multiply_reduce_fusion.1
  235.2 1.7 convert_reduce_fusion
  237.9 9.8 %all-to-all-start.1 = ((f32[16,1,1536]{2,1,0:T(1,128)}), f32[16,1,1536]{2,1,0:T(1,128)S(1)}, u32[]{:S(2)}, u32[]{:S(2)}) async-start(f32[16,1,1536]{2,1,0:T(1,128)} %reshape.342), calls=%async_computation.1 | async-start | bytes 196608 | tf_op jit(solution)/shard_map/all_to_all | solution.py:46
  249.4 100.0 %all-reduce.2 = (f32[1024]{0:T(1024)}, f32[1024]{0:T(1024)}, f32[12,225]{1,0:T(8,128)}) all-reduce(f32[1024]{0:T(1024)S(1)} %add.126, f32[1024]{0:T(1024)S(1)} %get-tuple-element.49, f32[12,225]{1,0:T(8,128)S(1)} %fusion.1), channel_id=1, replica_groups=mesh['row'=32,'col'=8,'dp'=2] {'row','col','dp'}, use_global_device_ids=true, to_apply=%region_12.13 | all-reduce | flops 4748 | bytes 37984 | tf_op jit(solution)/shard_map/psum | solution.py:270
  351.4 171.8 %all-reduce.5.cloned.1.call-done = f32[48,1024]{1,0:T(8,128)} async-done(((f32[48,1024]{1,0:T(8,128)}), f32[48,1024]{1,0:T(8,128)}) %all-reduce.5.cloned.1.call-update) | async-done | bytes 196624 | tf_op jit(solution)/shard_map/psum | solution.py:270
  523.3 1.6 copy.233
  (124 shorter events, 36.3 us)
Async XLA Ops:
  7.2 89.5 %copy-start = (bf16[48,1024]{1,0:T(8,128)(2,1)S(1)}, bf16[48,1024]{1,0:T(8,128)(2,1)}, u32[]{:S(2)}) copy-start(bf16[48,1024]{1,0:T(8,128)(2,1)} %param.12) | copy-start | bytes 294916
  7.2 58.1 %copy-start.12 = (bf16[1,3,32,128]{3,2,1,0:T(8,128)(2,1)S(1)}, bf16[1,3,32,128]{3,2,1,0:T(8,128)(2,1)}, u32[]{:S(2)}) copy-start(bf16[1,3,32,128]{3,2,1,0:T(8,128)(2,1)} %param.10) | copy-start | bytes 73732
  7.2 68.2 %copy-start.3 = (bf16[1,8,32,1024]{3,2,1,0:T(8,128)(2,1)S(1)}, bf16[1,8,32,1024]{3,2,1,0:T(8,128)(2,1)}, u32[]{:S(2)}) copy-start(bf16[1,8,32,1024]{3,2,1,0:T(8,128)(2,1)} %param.11) | copy-start | bytes 1572868
  7.2 124.9 %all-gather.4.cloned.1.call-start = ((), (), s32[]{:S(2)}) async-start(), calls=%async_computation.2 | async-start | bytes 4866048 | tf_op jit(solution)/shard_map/all_gather | solution.py:207
  63.6 16.3 %copy-start.19 = (s32[1,2]{1,0:T(1,128)S(1)}, s32[1,2]{1,0:T(1,128)}, u32[]{:S(2)}) copy-start(s32[1,2]{1,0:T(1,128)} %param.19) | copy-start | bytes 28
  63.6 18.4 %copy-start.14 = (s32[64,64]{1,0:T(8,128)S(1)}, s32[64,64]{1,0:T(8,128)}, u32[]{:S(2)}) copy-start(s32[64,64]{1,0:T(8,128)} %param.18) | copy-start | bytes 49156
  64.2 18.7 %copy-start.20 = (f32[12,225]{1,0:T(8,128)S(1)}, f32[12,225]{1,0:T(8,128)}, u32[]{:S(2)}) copy-start(f32[12,225]{1,0:T(8,128)} %param.17) | copy-start | bytes 32404
  65.2 137.2 %all-gather.6.cloned.1.call-start = ((), (), s32[]{:S(2)}) async-start(), calls=%async_computation.3 | async-start | bytes 1622016 | tf_op jit(solution)/shard_map/all_gather | solution.py:238
  65.3 21.8 %collective-permute-start = (bf16[1,3,32,128]{3,2,1,0:T(8,128)(2,1)S(1)}, bf16[1,3,32,128]{3,2,1,0:T(8,128)(2,1)S(1)}, u32[]{:S(2)}, u32[]{:S(2)}) collective-permute-start(bf16[1,3,32,128]{3,2,1,0:T(8,128)(2,1)S(1)} %copy-done.12), channel_id=1, source_target_pairs={{0,496},{16,0},{32,16},{48,32},{64,48},{80,64},{96,80},{112,96},{1... | collective-permute-start | bytes 73736 | tf_op jit(solution)/shard_map/ppermute | solution.py:30
  75.4 22.3 %collective-permute-start.2 = (bf16[1,8,32,1024]{3,2,1,0:T(8,128)(2,1)S(1)}, bf16[1,8,32,1024]{3,2,1,0:T(8,128)(2,1)}, u32[]{:S(2)}, u32[]{:S(2)}) collective-permute-start(bf16[1,8,32,1024]{3,2,1,0:T(8,128)(2,1)S(1)} %copy-done.3), channel_id=1, source_target_pairs={{0,496},{16,0},{32,16},{48,32},{64,48},{80,64},{96,80},{112,96},{1... | collective-permute-start | bytes 1572872 | tf_op jit(solution)/shard_map/ppermute | solution.py:30
  82.1 5.1 copy-start.16
  87.2 6.9 %collective-permute-start.1 = (bf16[1,3,32,32]{3,2,1,0:T(8,128)(2,1)S(1)}, bf16[1,3,32,32]{3,2,1,0:T(8,128)(2,1)S(1)}, u32[]{:S(2)}, u32[]{:S(2)}) collective-permute-start(bf16[1,3,32,32]{3,2,1,0:T(8,128)(2,1)S(1)} %bitcast.126), channel_id=1, source_target_pairs={{0,14},{2,0},{4,2},{6,4},{8,6},{10,8},{12,10},{14,12},{1,15},{3,1}... | collective-permute-start | bytes 18440 | tf_op jit(solution)/shard_map/ppermute | solution.py:30
  92.5 4.1 copy-start.18
  97.3 3.6 copy-start.15
  98.8 6.1 %collective-permute-start.3 = (bf16[1,8,8,1024]{3,2,1,0:T(8,128)(2,1)S(1)}, bf16[1,8,8,1024]{3,2,1,0:T(8,128)(2,1)S(1)}, u32[]{:S(2)}, u32[]{:S(2)}) collective-permute-start(bf16[1,8,8,1024]{3,2,1,0:T(8,128)(2,1)S(1)} %slice.121), channel_id=1, source_target_pairs={{0,14},{2,0},{4,2},{6,4},{8,6},{10,8},{12,10},{14,12},{1,15},{3,1}... | collective-permute-start | bytes 393224 | tf_op jit(solution)/shard_map/ppermute | solution.py:30
  138.5 2.6 copy-start.5
  144.9 1.6 copy-start.1
  156.2 46.3 %copy-start.4 = (bf16[1,4,8,8,1024]{4,3,2,1,0:T(8,128)(2,1)S(1)}, bf16[1,4,8,8,1024]{4,3,2,1,0:T(8,128)(2,1)}, u32[]{:S(2)}) copy-start(bf16[1,4,8,8,1024]{4,3,2,1,0:T(8,128)(2,1)} %copy.180) | copy-start | bytes 1572868
  156.2 79.0 %all-to-all-start = ((bf16[32,24,1024]{2,1,0:T(8,128)(2,1)}), bf16[32,24,1024]{2,1,0:T(8,128)(2,1)}, u32[]{:S(2)}, u32[]{:S(2)}) async-start(bf16[32,24,1024]{2,1,0:T(8,128)(2,1)} %bitcast.113), calls=%async_computation | async-start | bytes 3145728 | tf_op jit(solution)/shard_map/all_to_all | solution.py:40
  209.5 2.6 copy-start.6
  209.5 2.6 copy-start.2
  222.8 2.8 copy-start.7
  228.2 1.1 copy-start.9
  228.2 1.1 copy-start.10
  233.4 0.9 copy-start.8
  233.4 0.9 copy-start.13
  235.2 12.6 %copy-start.11 = (f32[12,4096]{1,0:T(8,128)S(1)}, f32[12,4096]{1,0:T(8,128)}, u32[]{:S(2)}) copy-start(f32[12,4096]{1,0:T(8,128)} %reshape.216) | copy-start | bytes 589828
  235.2 12.6 %copy-start.17 = (s32[4096]{0:T(1024)S(1)}, s32[4096]{0:T(1024)}, u32[]{:S(2)}) copy-start(s32[4096]{0:T(1024)} %copy-done.16) | copy-start | bytes 49156
  237.9 111.5 %all-to-all-start.1 = ((f32[16,1,1536]{2,1,0:T(1,128)}), f32[16,1,1536]{2,1,0:T(1,128)S(1)}, u32[]{:S(2)}, u32[]{:S(2)}) async-start(f32[16,1,1536]{2,1,0:T(1,128)} %reshape.342), calls=%async_computation.1 | async-start | bytes 196608 | tf_op jit(solution)/shard_map/all_to_all | solution.py:46
  247.7 275.5 %all-reduce.5.cloned.1.call-start = ((), (), s32[]{:S(2)}) async-start(), calls=%async_computation.4 | async-start | bytes 393216 | tf_op jit(solution)/shard_map/psum | solution.py:270
Sparse Core Ops, SparseCore 0:
  65.4 66.7 all-gather.3
  134.3 68.1 all-gather.5
  254.1 269.1 all-reduce.4
where the time goes:
time: 532 us; the launch traced here: 531 us
  waiting for transfers between devices  241 us (45%)
  blocking collectives  155 us (29%)
  local copies, waits for them, and re-layouts  41.8 us (8%)
  matrix products  32 us (6%)
  starting transfers between devices  31.2 us (6%)
  between operations  20.9 us (4%)
  other arithmetic  9.74 us (2%)
    psum x1, waiting for transfers between devices, on_device(): lax.psum((embed_grad, bias_grad, gain_contribution, table_grad), ('row',...  172 us
    psum x1, blocking collectives, on_device(): lax.psum((embed_grad, bias_grad, gain_contribution, table_grad), ('row',...  100 us
    all_gather x1, blocking collectives, gather_together(): lines, at, gathered = (lax.all_gather(line, axis), 0, [])  54.6 us
    all_gather x1, waiting for transfers between devices, on_device(): lax.all_gather(out_columns, 'row', axis=0, tiled=True)  41 us
    all_gather x1, waiting for transfers between devices, on_device(): qkv_full = lax.all_gather(qkv_columns, 'row', axis=0, tiled=True)  26.1 us
    ppermute x4, starting transfers between devices, from_behind(): return lax.ppermute(value, axis, pairs)  16 us
  transfers between devices with their start and end apart: 9, of which 4 were waited for; matrix products, arithmetic and copies ran while one was open for 14% of the time, Pallas kernels for 0%

commit v1 on v0

--- a/solution.py
+++ b/solution.py
@@ -1,3 +1,4 @@
+import functools
 import jax
 import jax.numpy as jnp
 from jax import lax
@@ -6,6 +7,15 @@
 WIN = 8
 PATCH = 4
 norm_epsilon = 1e-05
+
+
+def begin_field(vec, ndim_at):
+    block_out = jnp.stack([vec for _ in range(lax.axis_size("row"))])
+    current_block = lax.all_to_all(block_out, "row", 0, 0)
+    return jnp.concatenate(current_block, ndim_at)
+
+
+answer_the_lines = functools.partial(begin_field, ndim_at=0)
 
 
 def laid_out(blocks, dim):
@@ -235,7 +245,7 @@
     )
     d_attended = lax.dot_general(
         cot_flat,
-        lax.all_gather(out_columns, "row", axis=0, tiled=True),
+        answer_the_lines(out_columns),
         (((1,), (1,)), ((), ())),
         preferred_element_type=jnp.float32,
     ).astype(jnp.bfloat16)

time: 532 us -> 515 us (0.968)
  waiting for transfers between devices: 241 us -> 215 us
  starting transfers between devices: 31.2 us -> 37.8 us
    all_gather x1 -> x0, waiting for transfers between devices: 41 us -> none  [on_device(): lax.all_gather(out_columns, 'row', axis=0, tiled=True)]
    all_gather x1, waiting for transfers between devices: 26.1 us -> 35.8 us  [on_device(): qkv_full = lax.all_gather(qkv_columns, 'row', axis=0, tiled=True)]
    all_to_all x0 -> x1, starting transfers between devices: none -> 7.61 us  [begin_field(): current_block = lax.all_to_all(block_out, 'row', 0, 0)]
  transfers between devices with their start and end apart: 9 -> 9, of which waited for: 4 -> 4; matrix products, arithmetic and copies ran while one was open for 14% -> 15% of each run, Pallas kernels for 0% -> 0%
where the time goes in v1:
time: 515 us; the launch traced here: 514 us
  waiting for transfers between devices  215 us (42%)
  blocking collectives  155 us (30%)
  local copies, waits for them, and re-layouts  42.5 us (8%)
  starting transfers between devices  37.8 us (7%)
  matrix products  32 us (6%)
  between operations  21.2 us (4%)
  other arithmetic  9.69 us (2%)
    psum x1, waiting for transfers between devices, on_device(): lax.psum((embed_grad, bias_grad, gain_contribution, table_grad), ('row',...  173 us
    psum x1, blocking collectives, on_device(): lax.psum((embed_grad, bias_grad, gain_contribution, table_grad), ('row',...  100 us
    all_gather x1, blocking collectives, gather_together(): lines, at, gathered = (lax.all_gather(line, axis), 0, [])  54.6 us
    all_gather x1, waiting for transfers between devices, on_device(): qkv_full = lax.all_gather(qkv_columns, 'row', axis=0, tiled=True)  35.8 us
    ppermute x4, starting transfers between devices, from_behind(): return lax.ppermute(value, axis, pairs)  16 us
  transfers between devices with their start and end apart: 9, of which 4 were waited for; matrix products, arithmetic and copies ran while one was open for 15% of the time, Pallas kernels for 0%

profile of v1, /device:TPU:1, one launch (start us, length us, event | category | flops | bytes accessed | tf_op | source)
XLA Modules:
  0.0 513.5 jit_solution(8833612063550582381)
XLA Ops:
  8.9 54.6 %all-gather = bf16[98304]{0:T(1024)(128)(2,1)S(1)} all-gather(bf16[6144]{0:T(1024)(128)(2,1)S(1)} %pad_maximum_fusion), channel_id=2, replica_groups=mesh['row'=32,'col'=8,'dp'=2] {'col','dp'}, dimensions={0}, use_global_device_ids=true | all-gather | bytes 208896 | tf_op jit(solution)/shard_map/all_gather | solution.py:29
  65.2 10.1 %collective-permute-start = (bf16[1,3,32,128]{3,2,1,0:T(8,128)(2,1)S(1)}, bf16[1,3,32,128]{3,2,1,0:T(8,128)(2,1)S(1)}, u32[]{:S(2)}, u32[]{:S(2)}) collective-permute-start(bf16[1,3,32,128]{3,2,1,0:T(8,128)(2,1)S(1)} %copy-done.12), channel_id=1, source_target_pairs={{0,496},{16,0},{32,16},{48,32},{64,48},{80,64},{96,80},{112,96},{1... | collective-permute-start | bytes 73736 | tf_op jit(solution)/shard_map/ppermute | solution.py:40
  75.3 1.9 collective-permute-start.2
  79.0 7.6 %all-to-all-start.2 = ((bf16[32,24,1024]{2,1,0:T(8,128)(2,1)}), bf16[32,24,1024]{2,1,0:T(8,128)(2,1)}, u32[]{:S(2)}, u32[]{:S(2)}) async-start(bf16[32,24,1024]{2,1,0:T(8,128)(2,1)} %stack.3), calls=%async_computation.2 | async-start | bytes 3145728 | tf_op jit(solution)/shard_map/all_to_all | solution.py:14
  86.6 1.7 reshape.210
  91.2 2.6 convolution_bitcast_fusion
  95.6 1.9 collective-permute-start.1
  102.6 1.7 reshape.198
  107.1 2.1 collective-permute-start.3
  111.0 2.8 collective-permute-done.3
  114.9 35.8 %all-gather.3.cloned.1.call-done = bf16[1024,2304]{1,0:T(8,128)(2,1)} async-done(((bf16[32,2304]{1,0:T(8,128)(2,1)}), bf16[1024,2304]{1,0:T(8,128)(2,1)}) %all-gather.3.cloned.1.call-update) | async-done | bytes 4718608 | tf_op jit(solution)/shard_map/all_gather | solution.py:217
  150.6 3.9 convolution_convert_fusion
  157.0 2.6 reshape.340
  161.2 1.8 copy.192
  163.4 1.6 fusion.42
  165.1 3.8 fusion.7
  168.8 1.8 copy.179
  171.8 2.9 convolution_convert_fusion.1
  174.7 5.5 %all-to-all-start = ((bf16[32,24,1024]{2,1,0:T(8,128)(2,1)}), bf16[32,24,1024]{2,1,0:T(8,128)(2,1)}, u32[]{:S(2)}, u32[]{:S(2)}) async-start(bf16[32,24,1024]{2,1,0:T(8,128)(2,1)} %bitcast.114), calls=%async_computation | async-start | bytes 3145728 | tf_op jit(solution)/shard_map/all_to_all | solution.py:50
  180.2 2.8 convolution_convert_fusion.4
  183.0 2.4 reshape.343
  185.4 1.8 copy.196
  187.3 2.5 multiply_reduce_fusion
  191.1 1.9 copy.200
  193.0 1.8 reshape.218
  203.4 2.5 fusion.8
  207.1 4.0 multiply_reduce_fusion.1
  212.9 4.2 all-to-all-done
  217.1 1.7 convert_reduce_fusion
  219.8 8.6 %all-to-all-start.1 = ((f32[16,1,1536]{2,1,0:T(1,128)}), f32[16,1,1536]{2,1,0:T(1,128)S(1)}, u32[]{:S(2)}, u32[]{:S(2)}) async-start(f32[16,1,1536]{2,1,0:T(1,128)} %reshape.344), calls=%async_computation.1 | async-start | bytes 196608 | tf_op jit(solution)/shard_map/all_to_all | solution.py:56
  230.0 100.3 %all-reduce.2 = (f32[1024]{0:T(1024)}, f32[1024]{0:T(1024)}, f32[12,225]{1,0:T(8,128)}) all-reduce(f32[1024]{0:T(1024)S(1)} %add.126, f32[1024]{0:T(1024)S(1)} %get-tuple-element.49, f32[12,225]{1,0:T(8,128)S(1)} %fusion.1), channel_id=1, replica_groups=mesh['row'=32,'col'=8,'dp'=2] {'row','col','dp'}, use_global_device_ids=true, to_apply=%region_12.13 | all-reduce | flops 4748 | bytes 37984 | tf_op jit(solution)/shard_map/psum | solution.py:280
  332.5 172.6 %all-reduce.5.cloned.1.call-done = f32[48,1024]{1,0:T(8,128)} async-done(((f32[48,1024]{1,0:T(8,128)}), f32[48,1024]{1,0:T(8,128)}) %all-reduce.5.cloned.1.call-update) | async-done | bytes 196624 | tf_op jit(solution)/shard_map/psum | solution.py:280
  (124 shorter events, 38.7 us)
Async XLA Ops:
  7.2 97.8 %copy-start = (bf16[48,1024]{1,0:T(8,128)(2,1)S(1)}, bf16[48,1024]{1,0:T(8,128)(2,1)}, u32[]{:S(2)}) copy-start(bf16[48,1024]{1,0:T(8,128)(2,1)} %param.12) | copy-start | bytes 294916
  7.2 58.0 %copy-start.12 = (bf16[1,3,32,128]{3,2,1,0:T(8,128)(2,1)S(1)}, bf16[1,3,32,128]{3,2,1,0:T(8,128)(2,1)}, u32[]{:S(2)}) copy-start(bf16[1,3,32,128]{3,2,1,0:T(8,128)(2,1)} %param.10) | copy-start | bytes 73732
  7.2 68.1 %copy-start.3 = (bf16[1,8,32,1024]{3,2,1,0:T(8,128)(2,1)S(1)}, bf16[1,8,32,1024]{3,2,1,0:T(8,128)(2,1)}, u32[]{:S(2)}) copy-start(bf16[1,8,32,1024]{3,2,1,0:T(8,128)(2,1)} %param.11) | copy-start | bytes 1572868
  7.2 143.4 %all-gather.3.cloned.1.call-start = ((), (), s32[]{:S(2)}) async-start(), calls=%async_computation.3 | async-start | bytes 4866048 | tf_op jit(solution)/shard_map/all_gather | solution.py:217
  65.2 30.3 %collective-permute-start = (bf16[1,3,32,128]{3,2,1,0:T(8,128)(2,1)S(1)}, bf16[1,3,32,128]{3,2,1,0:T(8,128)(2,1)S(1)}, u32[]{:S(2)}, u32[]{:S(2)}) collective-permute-start(bf16[1,3,32,128]{3,2,1,0:T(8,128)(2,1)S(1)} %copy-done.12), channel_id=1, source_target_pairs={{0,496},{16,0},{32,16},{48,32},{64,48},{80,64},{96,80},{112,96},{1... | collective-permute-start | bytes 73736 | tf_op jit(solution)/shard_map/ppermute | solution.py:40
  75.3 30.7 %collective-permute-start.2 = (bf16[1,8,32,1024]{3,2,1,0:T(8,128)(2,1)S(1)}, bf16[1,8,32,1024]{3,2,1,0:T(8,128)(2,1)}, u32[]{:S(2)}, u32[]{:S(2)}) collective-permute-start(bf16[1,8,32,1024]{3,2,1,0:T(8,128)(2,1)S(1)} %copy-done.3), channel_id=1, source_target_pairs={{0,496},{16,0},{32,16},{48,32},{64,48},{80,64},{96,80},{112,96},{1... | collective-permute-start | bytes 1572872 | tf_op jit(solution)/shard_map/ppermute | solution.py:40
  78.9 9.3 %copy-start.19 = (s32[1,2]{1,0:T(1,128)S(1)}, s32[1,2]{1,0:T(1,128)}, u32[]{:S(2)}) copy-start(s32[1,2]{1,0:T(1,128)} %param.19) | copy-start | bytes 28
  78.9 11.4 %copy-start.14 = (s32[64,64]{1,0:T(8,128)S(1)}, s32[64,64]{1,0:T(8,128)}, u32[]{:S(2)}) copy-start(s32[64,64]{1,0:T(8,128)} %param.18) | copy-start | bytes 49156
  79.0 95.7 %all-to-all-start.2 = ((bf16[32,24,1024]{2,1,0:T(8,128)(2,1)}), bf16[32,24,1024]{2,1,0:T(8,128)(2,1)}, u32[]{:S(2)}, u32[]{:S(2)}) async-start(bf16[32,24,1024]{2,1,0:T(8,128)(2,1)} %stack.3), calls=%async_computation.2 | async-start | bytes 3145728 | tf_op jit(solution)/shard_map/all_to_all | solution.py:14
  86.6 4.7 copy-start.20
  90.4 5.1 copy-start.16
  95.6 6.9 %collective-permute-start.1 = (bf16[1,3,32,32]{3,2,1,0:T(8,128)(2,1)S(1)}, bf16[1,3,32,32]{3,2,1,0:T(8,128)(2,1)S(1)}, u32[]{:S(2)}, u32[]{:S(2)}) collective-permute-start(bf16[1,3,32,32]{3,2,1,0:T(8,128)(2,1)S(1)} %bitcast.127), channel_id=1, source_target_pairs={{0,14},{2,0},{4,2},{6,4},{8,6},{10,8},{12,10},{14,12},{1,15},{3,1}... | collective-permute-start | bytes 18440 | tf_op jit(solution)/shard_map/ppermute | solution.py:40
  100.8 4.1 copy-start.18
  105.6 3.6 copy-start.15
  107.1 6.6 %collective-permute-start.3 = (bf16[1,8,8,1024]{3,2,1,0:T(8,128)(2,1)S(1)}, bf16[1,8,8,1024]{3,2,1,0:T(8,128)(2,1)S(1)}, u32[]{:S(2)}, u32[]{:S(2)}) collective-permute-start(bf16[1,8,8,1024]{3,2,1,0:T(8,128)(2,1)S(1)} %slice.121), channel_id=1, source_target_pairs={{0,14},{2,0},{4,2},{6,4},{8,6},{10,8},{12,10},{14,12},{1,15},{3,1}... | collective-permute-start | bytes 393224 | tf_op jit(solution)/shard_map/ppermute | solution.py:40
  157.0 2.6 copy-start.5
  163.4 1.6 copy-start.1
  174.7 5.5 %copy-start.4 = (bf16[1,4,8,8,1024]{4,3,2,1,0:T(8,128)(2,1)S(1)}, bf16[1,4,8,8,1024]{4,3,2,1,0:T(8,128)(2,1)}, u32[]{:S(2)}) copy-start(bf16[1,4,8,8,1024]{4,3,2,1,0:T(8,128)(2,1)} %copy.180) | copy-start | bytes 1572868
  174.7 42.5 %all-to-all-start = ((bf16[32,24,1024]{2,1,0:T(8,128)(2,1)}), bf16[32,24,1024]{2,1,0:T(8,128)(2,1)}, u32[]{:S(2)}, u32[]{:S(2)}) async-start(bf16[32,24,1024]{2,1,0:T(8,128)(2,1)} %bitcast.114), calls=%async_computation | async-start | bytes 3145728 | tf_op jit(solution)/shard_map/all_to_all | solution.py:50
  187.2 2.5 copy-start.6
  187.2 2.5 copy-start.2
  200.6 2.8 copy-start.7
  205.9 1.1 copy-start.9
  205.9 1.1 copy-start.10
  211.1 0.9 copy-start.8
  211.1 0.9 copy-start.13
  212.9 15.5 %copy-start.11 = (f32[12,4096]{1,0:T(8,128)S(1)}, f32[12,4096]{1,0:T(8,128)}, u32[]{:S(2)}) copy-start(f32[12,4096]{1,0:T(8,128)} %reshape.218) | copy-start | bytes 589828
  212.9 15.5 %copy-start.17 = (s32[4096]{0:T(1024)S(1)}, s32[4096]{0:T(1024)}, u32[]{:S(2)}) copy-start(s32[4096]{0:T(1024)} %copy-done.16) | copy-start | bytes 49156
  219.8 110.6 %all-to-all-start.1 = ((f32[16,1,1536]{2,1,0:T(1,128)}), f32[16,1,1536]{2,1,0:T(1,128)S(1)}, u32[]{:S(2)}, u32[]{:S(2)}) async-start(f32[16,1,1536]{2,1,0:T(1,128)} %reshape.344), calls=%async_computation.1 | async-start | bytes 196608 | tf_op jit(solution)/shard_map/all_to_all | solution.py:56
  228.4 276.7 %all-reduce.5.cloned.1.call-start = ((), (), s32[]{:S(2)}) async-start(), calls=%async_computation.4 | async-start | bytes 393216 | tf_op jit(solution)/shard_map/psum | solution.py:280
Sparse Core Ops, SparseCore 0:
  65.3 85.2 all-gather.2
  234.8 270.2 all-reduce.4
